TPU v7x, 32 devices: a whole 2x2x4 slice. The times are simulated.
32 devices in a mesh: rep: 2 (over y), seq: 4 (over z), head: 2 (over x), sub: 2 (over core).
Axes of the slice: x: 2, y: 2, z: 4, core: 2. Of those that a mesh axis runs over, the one named last changes fastest.
Arguments:
- queries: bfloat16 [8, 8192], P('rep', 'head'), parts along dimension 0, may hold values from -4.5 to 4.5
- key_cache: bfloat16 [1024, 128, 1024], P(('rep', 'seq', 'sub'), None, 'head'), parts along dimension 0, may hold values from -4.5 to 4.5
- value_cache: bfloat16 [1024, 128, 1024], P(('rep', 'seq', 'sub'), None, 'head'), parts along dimension 0, may hold values from -6 to 6
- seq_lengths: int32 [8], P('rep'), parts along dimension 0, may hold values from 513 to 32768, as said below
- slot_owner: int32 [1024], P(('rep', 'seq', 'sub')), parts along dimension 0, may hold values from 0 to 3, as said below
- slot_page: int32 [1024], P(('rep', 'seq', 'sub')), parts along dimension 0, may hold values from 0 to 255, as said below
- out_weight: bfloat16 [8192, 8192], P('head', ('seq', 'sub')), may hold values from -0.0625 to 0.0625
Outputs:
- projected: bfloat16 [8, 8192], P('rep', ('seq', 'sub')), parts along dimension 0
There are 2 independent parts, one for each index of `rep`. A program takes and returns all parts, laid end to end along the dimension named above; an argument that names none is the same for every part. Nothing has to cross between parts.
Inputs may be any that keep to these rules, and one draw needn't show every extreme that they name: `slot_owner`: every sequence holds 5 to 256 pages, and some sequence exactly 256; its pages are numbered 0 upward and each stands in exactly one cache page; every cache page is used; a sequence's pages occupy consecutive cache pages. slot_page[s] < ceil(seq_lengths[slot_owner[s]] / 128), and every page below that count is present. seq_lengths[b] lies in the last of its sequence's pages.
All inputs are finite; a program needn't handle non-finite values.
Results may differ from a plain program's by a relative error of at most 0.0055.
Values may be sent and summed in bfloat16 or wider, within the bound.
A program may use at most 64 MiB of HBM per device.

v0:
```python
import jax
import jax.numpy as jnp
from jax import lax
from jax.sharding import PartitionSpec as P

DH = 128
PAGE = 128


neg_fill = -1e30


def merged(part, axis, combine):
    gathered = jax.tree.map(lambda a: lax.all_gather(a, axis), part)

    def take(source):
        return jax.tree.map(lambda a: lax.dynamic_index_in_dim(a, source, 0, False), gathered)

    return lax.fori_loop(
        1, lax.axis_size(axis), lambda source, state: combine(state, take(source)), take(0)
    )


def spread(values, factor):
    row_count, col_count = factor.shape
    return (values.reshape(row_count, col_count, -1) * factor[:, :, None]).reshape(row_count, -1)


def merge_states(first, second):
    top_first, mass_first, out_first = first
    top_second, mass_second, out_second = second
    joined = jnp.maximum(top_first, top_second)
    scale_first = jnp.exp(top_first - joined)
    scale_second = jnp.exp(top_second - joined)
    mass_joined = mass_first * scale_first + mass_second * scale_second
    out_joined = spread(out_first, scale_first) + spread(out_second, scale_second)
    return (joined, mass_joined, out_joined)


def on_device(queries, key_cache, value_cache, seq_lengths, slot_owner, slot_page, out_weight):
    batch_rows = queries.shape[0]
    slot_count = key_cache.shape[0]
    groups_local = key_cache.shape[2] // DH
    per_group = queries.shape[1] // (groups_local * DH)
    picked = jnp.take(queries, slot_owner, axis=0).reshape(slot_count, groups_local, per_group, DH)
    key_tiles = key_cache.reshape(slot_count, PAGE, groups_local, DH)
    value_tiles = value_cache.reshape(slot_count, PAGE, groups_local, DH)
    scores = jnp.einsum("sgjd,stgd->sgjt", picked, key_tiles, preferred_element_type=jnp.float32)
    scores = scores * (1.0 / jnp.sqrt(jnp.float32(DH)))
    valid = jnp.clip(jnp.take(seq_lengths, slot_owner, axis=0) - slot_page * PAGE, 0, PAGE)
    positions = jnp.arange(PAGE, dtype=jnp.int32)
    live = (positions[None, :] < valid[:, None])[:, None, None, :]
    scores = jnp.where(live, scores, neg_fill)
    page_peak = jnp.max(scores, axis=-1)
    probs = jnp.exp(scores - page_peak[..., None]).astype(jnp.bfloat16)
    page_mass = jnp.sum(probs.astype(jnp.float32), axis=-1)
    page_out = jnp.einsum("sgjt,stgd->sgjd", probs, value_tiles, preferred_element_type=jnp.float32)
    owner_hits = slot_owner[None, :] == jnp.arange(batch_rows, dtype=jnp.int32)[:, None]
    seq_peak = jnp.max(jnp.where(owner_hits[:, :, None, None], page_peak[None], neg_fill), axis=1)
    factor = jnp.exp(page_peak - jnp.take(seq_peak, slot_owner, axis=0))
    hit_float = owner_hits.astype(jnp.float32)
    heads_local = groups_local * per_group
    seq_mass = jnp.dot(
        hit_float,
        (page_mass * factor).reshape(slot_count, heads_local),
        precision=lax.Precision.HIGHEST,
        preferred_element_type=jnp.float32,
    )
    seq_out = jnp.dot(
        hit_float,
        (page_out * factor[..., None]).reshape(slot_count, heads_local * DH),
        precision=lax.Precision.HIGHEST,
        preferred_element_type=jnp.float32,
    )
    seq_peak = seq_peak.reshape(batch_rows, heads_local)
    top_all, mass_all, out_all = merged((seq_peak, seq_mass, seq_out), ("seq", "sub"), merge_states)
    attention = spread(out_all, 1.0 / mass_all).astype(jnp.bfloat16)
    partial_out = jnp.dot(attention, out_weight, preferred_element_type=jnp.float32)
    return lax.psum(partial_out, "head").astype(jnp.bfloat16)


def solution(mesh):
    in_specs = (
        P("rep", "head"),
        P(("rep", "seq", "sub"), None, "head"),
        P(("rep", "seq", "sub"), None, "head"),
        P("rep"),
        P(("rep", "seq", "sub")),
        P(("rep", "seq", "sub")),
        P("head", ("seq", "sub")),
    )
    out_specs = P("rep", ("seq", "sub"))
    return jax.shard_map(
        on_device, mesh=mesh, in_specs=in_specs, out_specs=out_specs, check_vma=False
    )
```

profile of v0, /device:TPU:0, one launch (start us, length us, event | category | flops | bytes accessed | tf_op | source)
XLA Modules:
  0.0 78.8 jit_solution(3403634785775584727)
XLA Ops:
  0.0 0.0 copy-start
  0.0 0.0 copy-start.1
  0.0 1.5 %fusion.40 = (s32[1]{0:T(128)}, s32[1]{0:T(128)}, s32[1]{0:T(128)}, s32[1]{0:T(128)}) fusion(s32[4]{0:T(128)} %param.12), kind=kLoop, calls=%fused_computation.62 | loop fusion | bytes 32 | tf_op jit(solution)/shard_map/jit(_take)/gather | solution.py:50
  1.5 3.2 %fusion.36 = (s32[64]{0:T(128)S(1)}, s32[64]{0:T(128)S(1)}) fusion(s32[64]{0:T(128)} %param.14, s32[]{:T(128)} %bitcast.3, s32[]{:T(128)} %bitcast.4, s32[]{:T(128)} %bitcast.5, s32[]{:T(128)} %bitcast.6, s32[64]{0:T(128)} %param.13), kind=kLoop, calls=%fused_computation.59 | loop fusion | flops 1024 | bytes 1040 | tf_op jit(solution)/shard_map/jit(clip)/min | solution.py:50
  4.7 0.0 copy-done
  4.7 0.8 %gather_fusion = bf16[64,4096]{1,0:T(8,128)(2,1)S(1)} fusion(bf16[4,4096]{1,0:T(4,128)(2,1)S(1)} %copy-done, s32[1024]{0:T(1024)S(1)} %pad_clamp_fusion), kind=kCustom, calls=%fused_computation | custom fusion | bytes 1048832 | tf_op jit(solution)/shard_map/jit(_take)/gather | solution.py:45
  5.5 0.1 copy.34
  5.6 0.7 compare_and_fusion
  6.3 0.1 iota_compare_fusion
  6.3 7.0 %fusion.41 = (f32[64,4,8]{2,1,0:T(4,128)S(1)}, f32[64,4,8,128]{3,2,1,0:T(8,128)S(1)}) fusion(bf16[64,4,8,128]{3,2,1,0:T(8,128)(2,1)S(1)} %bitcast.106, pred[64]{0:T(512)(128)(4,1)S(1)} %compare_and_fusion, pred[64,128]{1,0:T(8,128)(4,1)S(1)} %iota_compare_fusion, bf16[64,128,512]{2,1,0:T(8,128)(2,1)} %param.10), kind=kOutput, calls=%fused_computation.63 | convolution fusion | flops 68155392 | bytes 9977920 | tf_op jit(solution)/shard_map/sgjd,stgd->sgjt/dot_general | solution.py:48
  13.4 0.1 copy.25
  13.5 0.0 copy-done.1
  13.5 0.1 select_reduce_fusion
  13.6 0.1 all_gather_reshape.3
  13.7 14.5 %all_gather.15 = f32[8,4,32]{2,1,0:T(4,128)S(1)} all-gather(f32[1,4,32]{2,1,0:T(4,128)S(1)} %all_gather_reshape.3), channel_id=1, replica_groups=mesh['rep'=2,'seq'=4,'head'=2,'sub'=2] {'seq','sub'}, dimensions={0}, use_global_device_ids=true | all-gather | bytes 4608 | tf_op jit(solution)/shard_map/all_gather | solution.py:14
  28.2 0.7 gather_fusion.1
  28.8 0.1 copy.28
  28.9 0.8 convert_reduce_fusion
  29.7 0.1 copy.26
  29.8 0.1 convolution_bitcast_fusion.1
  29.9 12.8 %all-gather.2 = f32[8,4,32]{2,1,0:T(4,128)S(1)} all-gather(f32[1,4,32]{2,1,0:T(4,128)S(1)} %convolution_bitcast_fusion.1), channel_id=2, replica_groups=mesh['rep'=2,'seq'=4,'head'=2,'sub'=2] {'seq','sub'}, dimensions={0}, use_global_device_ids=true | all-gather | bytes 4608 | tf_op jit(solution)/shard_map/all_gather | solution.py:14
  42.7 0.1 subtract_exponential_fusion.1
  42.8 4.7 %fusion.12 = f32[64,4,8,128]{3,2,1,0:T(8,128)S(1)} fusion(f32[64,4,8]{2,1,0:T(4,128)S(1)} %subtract_exponential_fusion.1, f32[64,4,8,128]{3,2,1,0:T(8,128)S(1)} %get-tuple-element.211, f32[64,4,8]{2,1,0:T(4,128)S(1)} %get-tuple-element.210, bf16[64,128,512]{2,1,0:T(8,128)(2,1)} %param.11), kind=kOutput, calls=%fused_computation.21 | convolution fusion | flops 67895296 | bytes 10502144 | tf_op jit(solution)/shard_map/sgjt,stgd->sgjd/dot_general | solution.py:57
  47.6 1.0 %convolution_bitcast_fusion = f32[1,4,4096]{2,1,0:T(4,128)S(1)} fusion(f32[8,8,32,128]{3,2,1,0:T(8,128)S(1)} %bitcast.108, s32[64]{0:T(128)S(1)} %copy-done.1), kind=kOutput, calls=%fused_computation.19 | convolution fusion | flops 12583168 | bytes 1114368 | tf_op jit(solution)/shard_map/dot_general | solution.py:69
  48.6 14.9 %all-gather.3 = f32[8,4,4096]{2,1,0:T(4,128)S(1)} all-gather(f32[1,4,4096]{2,1,0:T(4,128)S(1)} %convolution_bitcast_fusion), channel_id=3, replica_groups=mesh['rep'=2,'seq'=4,'head'=2,'sub'=2] {'seq','sub'}, dimensions={0}, use_global_device_ids=true | all-gather | bytes 589824 | tf_op jit(solution)/shard_map/all_gather | solution.py:14
  63.5 1.9 %while.19 = (s32[]{:T(128)}, f32[4,32]{1,0:T(4,128)S(1)}, f32[4,32]{1,0:T(4,128)S(1)}, f32[4,4096]{1,0:T(4,128)S(1)}, f32[8,4,32]{2,1,0:T(4,128)S(1)}, /*index=5...) while((s32[]{:T(128)}, f32[4,32]{1,0:T(4,128)S(1)}, ...), condition=%wide.region_4.5_spmd, body=%wide.region_3.4_spmd.sunk | while | flops 49925 | bytes 464023 | solution.py:19
  63.6 0.1 broadcast_bitcast_fusion.4
  63.7 0.1 fusion.48
  63.8 0.1 broadcast_bitcast_fusion.4
  63.9 0.1 fusion.48
  64.1 0.1 broadcast_bitcast_fusion.4
  64.2 0.1 fusion.48
  64.4 0.1 broadcast_bitcast_fusion.4
  64.5 0.1 fusion.48
  64.6 0.1 broadcast_bitcast_fusion.4
  64.7 0.1 fusion.48
  64.9 0.1 broadcast_bitcast_fusion.4
  65.0 0.1 fusion.48
  65.2 0.1 broadcast_bitcast_fusion.4
  65.3 0.1 fusion.48
  65.4 0.1 broadcast_bitcast_fusion.2
  65.5 4.6 %fusion.24 = f32[4,1024]{1,0:T(4,128)S(1)} fusion(bf16[4096,1024]{1,0:T(8,128)(2,1)} %param.15, f32[4,4096]{1,0:T(4,128)S(1)} %get-tuple-element.182, f32[1,4,32,128]{3,2,1,0:T(8,128)S(1)} %broadcast_bitcast_fusion.2), kind=kOutput, calls=%fused_computation.36 | convolution fusion | flops 33587200 | bytes 8536064 | tf_op jit(solution)/shard_map/dot_general | solution.py:78
  70.1 8.7 %psum.7 = bf16[4,1024]{1,0:T(4,128)(2,1)} all-reduce(f32[4,1024]{1,0:T(4,128)S(1)} %fusion.24), channel_id=1, replica_groups=mesh['rep'=2,'seq'=4,'head'=2,'sub'=2] {'head'}, use_global_device_ids=true, to_apply=%region_5.6 | all-reduce | flops 4096 | bytes 24576 | tf_op jit(solution)/shard_map/psum | solution.py:79
  (13 shorter events, 0.2 us)
Async XLA Ops:
  0.0 4.7 %copy-start = (bf16[4,4096]{1,0:T(4,128)(2,1)S(1)}, bf16[4,4096]{1,0:T(4,128)(2,1)}, u32[]{:S(2)}) copy-start(bf16[4,4096]{1,0:T(4,128)(2,1)} %param.9) | copy-start | bytes 98308
  0.0 13.5 %copy-start.1 = (s32[64]{0:T(128)S(1)}, s32[64]{0:T(128)}, u32[]{:S(2)}) copy-start(s32[64]{0:T(128)} %param.13) | copy-start | bytes 772
where the time goes:
time: 79.1 us; the launch traced here: 78.8 us
  blocking collectives  50.9 us (64%)
  matrix products  17.5 us (22%)
  other arithmetic  6.07 us (8%)
  local copies, waits for them, and re-layouts  4.05 us (5%)
    all_gather x3, blocking collectives, merged(): gathered = jax.tree.map(lambda a: lax.all_gather(a, axis), part)  42.2 us
    psum x1, blocking collectives, on_device(): return lax.psum(partial_out, 'head').astype(jnp.bfloat16)  8.73 us
    dot_general x1, matrix products, on_device(): jnp.einsum('sgjd,stgd->sgjt', picked, key_tiles, preferred_element_type=j...  7.04 us
    dot_general x1, matrix products, on_device(): jnp.einsum('sgjt,stgd->sgjd', probs, value_tiles, preferred_element_type=...  4.72 us
    dot_general x1, matrix products, on_device(): jnp.dot(attention, out_weight, preferred_element_type=jnp.float32)  4.59 us
    min x1, other arithmetic, on_device(): jnp.clip(jnp.take(seq_lengths, slot_owner, axis=0) - slot_page * PAGE, 0,...  3.19 us

commit v1 on v0

v1 whole, which is shorter than its diff:
```python
import functools

import jax
import jax.numpy as jnp
from jax import lax
from jax.experimental import pallas as pl
from jax.experimental.pallas import tpu as pltpu
from jax.sharding import PartitionSpec as P

DH = 128
NEG = -1e30
MESH = pl.DeviceIdType.MESH


class Plan:
    def __init__(self, mesh_shape, q_shape, k_shape, w_shape):
        self.seq, self.sub, self.head = (mesh_shape[a] for a in ("seq", "sub", "head"))
        self.peers = self.seq * self.sub
        self.batch = q_shape[0]
        self.pages, self.page, self.width = k_shape
        self.groups = self.width // DH
        self.per_group = q_shape[1] // self.width
        self.unit_groups = 2 if self.groups % 2 == 0 else 1
        self.units = self.groups // self.unit_groups
        self.unit_heads = self.unit_groups * self.per_group
        self.unit_width = self.unit_groups * DH
        self.rows = self.batch * self.unit_heads
        self.lanes = max(128, self.rows)
        self.chunk = min(8, self.pages)
        self.chunks = self.pages // self.chunk
        self.span = self.chunk * self.page
        self.columns = w_shape[1]
        self.depth = self.unit_heads * DH


def kernel(
    pn,
    lengths, owners, numbers,
    q_ref, k_hbm, v_hbm, w_hbm,
    out_ref,
    kbuf, vbuf, wbuf, scores, qf, qb, att,
    osend, ssend, orecv, srecv, parts,
    ksem, vsem, wsem, osem_s, osem_r, ssem_s, ssem_r, psem_s, psem_r,
):
    i_seq, i_sub, i_head = (lax.axis_index(a) for a in ("seq", "sub", "head"))
    me = i_seq * pn.sub + i_sub
    n = pn.peers

    def peer_id(k):
        who = lax.rem(me + k, n)
        return {"seq": who // pn.sub, "sub": lax.rem(who, pn.sub)}

    def k_copy(u, c):
        at = (pl.ds(c * pn.chunk, pn.chunk), slice(None), pl.ds(u * pn.unit_width, pn.unit_width))
        return pltpu.make_async_copy(k_hbm.at[at], kbuf.at[at], ksem.at[u, c])

    def v_copy(u, c):
        at = (pl.ds(c * pn.chunk, pn.chunk), slice(None), pl.ds(u * pn.unit_width, pn.unit_width))
        return pltpu.make_async_copy(v_hbm.at[at], vbuf.at[at], vsem.at[u, c])

    def w_copy(u):
        at = pl.ds(u * pn.depth, pn.depth)
        return pltpu.make_async_copy(w_hbm.at[at], wbuf.at[at], wsem.at[u])

    for u in range(pn.units):
        for c in range(pn.chunks):
            k_copy(u, c).start()
        for c in range(pn.chunks):
            v_copy(u, c).start()
    for u in range(pn.units):
        w_copy(u).start()

    barrier = pltpu.get_barrier_semaphore()
    for k in range(1, n):
        pl.semaphore_signal(barrier, inc=1, device_id=peer_id(k), device_id_type=MESH)
    for k in range(1, pn.head):
        pl.semaphore_signal(
            barrier, inc=1, device_id={"head": lax.rem(i_head + k, pn.head)}, device_id_type=MESH
        )

    qf[...] = jnp.zeros_like(qf)
    for u in range(pn.units):
        for h in range(pn.unit_heads):
            g = h // pn.per_group
            col = (u * pn.unit_heads + h) * DH
            qf[u, g, pl.ds(h, pn.batch, stride=pn.unit_heads), :] = q_ref[
                :, pl.ds(col, DH)
            ].astype(jnp.float32)
    for u in range(pn.units):
        for g in range(pn.unit_groups):
            qb[u, :, pl.ds(g * DH, DH)] = qf[u, g].astype(jnp.bfloat16)
    scale = 1.0 / (DH**0.5)

    def o_copy(u, k):
        return pltpu.make_async_remote_copy(
            src_ref=osend.at[u], dst_ref=orecv.at[u, me],
            send_sem=osem_s.at[u, k], recv_sem=osem_r.at[u, k],
            device_id=peer_id(k), device_id_type=MESH,
        )

    def s_copy(u, k):
        return pltpu.make_async_remote_copy(
            src_ref=ssend.at[u], dst_ref=srecv.at[u, me],
            send_sem=ssem_s.at[u, k], recv_sem=ssem_r.at[u, k],
            device_id=peer_id(k), device_id_type=MESH,
        )

    def attend(u):
        cols = pl.ds(u * pn.unit_width, pn.unit_width)
        query = qb[u]
        spot = lax.broadcasted_iota(jnp.int32, (pn.unit_heads, pn.page), 1)

        def score_chunk(c, top):
            k_copy(u, c).wait()
            keys = kbuf[pl.ds(c * pn.chunk, pn.chunk), :, cols].reshape(pn.span, pn.unit_width)
            raw = lax.dot_general(
                query, keys, (((1,), (1,)), ((), ())), preferred_element_type=jnp.float32
            ) * scale
            pieces = []
            for p in range(pn.chunk):
                owner = owners[c * pn.chunk + p]
                number = numbers[c * pn.chunk + p]
                valid = jnp.clip(lengths[owner] - number * pn.page, 0, pn.page)
                blocks = []
                for b in range(pn.batch):
                    limit = jnp.where(owner == b, valid, 0)
                    part = raw[b * pn.unit_heads:(b + 1) * pn.unit_heads, p * pn.page:(p + 1) * pn.page]
                    blocks.append(jnp.where(spot < limit, part, NEG))
                piece = jnp.concatenate(blocks, axis=0)
                top = jnp.maximum(top, piece)
                pieces.append(piece)
            scores[c] = jnp.concatenate(pieces, axis=1)
            return top

        top = lax.fori_loop(
            0, pn.chunks, score_chunk, jnp.full((pn.rows, pn.page), NEG, jnp.float32)
        )
        peak = jnp.max(top, axis=1, keepdims=True)

        def value_chunk(c, state):
            mass, total = state
            v_copy(u, c).wait()
            probs = jnp.exp(scores[c] - peak).astype(jnp.bfloat16)
            values = vbuf[pl.ds(c * pn.chunk, pn.chunk), :, cols].reshape(pn.span, pn.unit_width)
            total = total + jnp.dot(probs, values, preferred_element_type=jnp.float32)
            pf = probs.astype(jnp.float32)
            for p in range(pn.chunk):
                mass = mass + pf[:, p * pn.page:(p + 1) * pn.page]
            return mass, total

        mass, total = lax.fori_loop(
            0, pn.chunks, value_chunk,
            (
                jnp.zeros((pn.rows, pn.page), jnp.float32),
                jnp.zeros((pn.rows, pn.unit_width), jnp.float32),
            ),
        )
        mass = jnp.sum(mass, axis=1, keepdims=True)
        level = peak + jnp.log(mass)
        blocks = []
        for b in range(pn.batch):
            for g in range(pn.unit_groups):
                r = b * pn.unit_heads + g * pn.per_group
                blocks.append(total[r:r + pn.per_group, g * DH:(g + 1) * DH])
        mine = (jnp.concatenate(blocks, axis=0) / mass).astype(jnp.bfloat16)
        line = jnp.transpose(jnp.broadcast_to(level, (pn.rows, 128)))[0:1, :]
        if pn.rows < pn.lanes:
            line = jnp.concatenate([line, jnp.zeros((1, pn.lanes - pn.rows), jnp.float32)], axis=1)
        ssend[u] = line
        osend[u] = mine
        srecv[u, me] = line
        orecv[u, me] = mine

    def send(u):
        for k in range(1, n):
            s_copy(u, k).start()
            o_copy(u, k).start()

    def merge(u):
        for k in range(1, n):
            s_copy(u, k).wait_recv()
        level = srecv[u].reshape(n, pn.lanes)
        weight = jnp.exp(level - jnp.max(level, axis=0, keepdims=True))
        weight = weight / jnp.sum(weight, axis=0, keepdims=True)
        turned = jnp.transpose(weight)
        for k in range(1, n):
            o_copy(u, k).wait_recv()
        total = None
        for s in range(n):
            term = orecv[u, s].astype(jnp.float32) * turned[0:pn.rows, s:s + 1]
            total = term if total is None else total + term
        att[u] = total
        heads = [att[u, pl.ds(h, pn.batch, stride=pn.unit_heads), :] for h in range(pn.unit_heads)]
        return jnp.concatenate(heads, axis=1).astype(jnp.bfloat16)

    for u in range(pn.units):
        attend(u)
        if u == 0:
            pl.semaphore_wait(barrier, n - 1 + pn.head - 1)
        send(u)

    total = jnp.zeros((pn.batch, pn.columns), jnp.float32)
    for u in range(pn.units):
        w_copy(u).wait()
        rows = merge(u)
        total = total + jnp.dot(
            rows, wbuf[pl.ds(u * pn.depth, pn.depth), :], preferred_element_type=jnp.float32
        )
    parts[i_head] = total

    def p_copy(k):
        return pltpu.make_async_remote_copy(
            src_ref=parts.at[i_head], dst_ref=parts.at[i_head],
            send_sem=psem_s.at[k], recv_sem=psem_r.at[k],
            device_id={"head": lax.rem(i_head + k, pn.head)}, device_id_type=MESH,
        )

    for k in range(1, pn.head):
        p_copy(k).start()
    for u in range(pn.units):
        for k in range(1, n):
            s_copy(u, k).wait_send()
            o_copy(u, k).wait_send()
    for k in range(1, pn.head):
        p_copy(k).wait()
    result = parts[0]
    for s in range(1, pn.head):
        result = result + parts[s]
    out_ref[...] = result.astype(out_ref.dtype)


def on_device(mesh_shape, queries, key_cache, value_cache, seq_lengths, slot_owner, slot_page, out_weight):
    pn = Plan(mesh_shape, queries.shape, key_cache.shape, out_weight.shape)
    smem = pl.BlockSpec(memory_space=pltpu.SMEM)
    vmem = pl.BlockSpec(memory_space=pltpu.VMEM)
    anywhere = pl.BlockSpec(memory_space=pl.ANY)
    n, u = pn.peers, pn.units
    dma = pltpu.SemaphoreType.DMA
    return pl.pallas_call(
        functools.partial(kernel, pn),
        out_shape=jax.ShapeDtypeStruct((pn.batch, pn.columns), queries.dtype),
        in_specs=[smem, smem, smem, vmem, anywhere, anywhere, anywhere],
        out_specs=vmem,
        scratch_shapes=[
            pltpu.VMEM(key_cache.shape, key_cache.dtype),
            pltpu.VMEM(value_cache.shape, value_cache.dtype),
            pltpu.VMEM(out_weight.shape, out_weight.dtype),
            pltpu.VMEM((pn.chunks, pn.rows, pn.span), jnp.float32),
            pltpu.VMEM((u, pn.unit_groups, pn.rows, DH), jnp.float32),
            pltpu.VMEM((u, pn.rows, pn.unit_width), jnp.bfloat16),
            pltpu.VMEM((u, pn.rows, DH), jnp.float32),
            pltpu.VMEM((u, pn.rows, DH), jnp.bfloat16),
            pltpu.VMEM((u, 1, pn.lanes), jnp.float32),
            pltpu.VMEM((u, n, pn.rows, DH), jnp.bfloat16),
            pltpu.VMEM((u, n, 1, pn.lanes), jnp.float32),
            pltpu.VMEM((pn.head, pn.batch, pn.columns), jnp.float32),
            dma((u, pn.chunks)), dma((u, pn.chunks)), dma((u,)),
            dma((u, n)), dma((u, n)), dma((u, n)), dma((u, n)),
            dma((pn.head,)), dma((pn.head,)),
        ],
        compiler_params=pltpu.CompilerParams(
            collective_id=0, has_side_effects=True, vmem_limit_bytes=60 * 1024 * 1024
        ),
    )(seq_lengths, slot_owner, slot_page, queries, key_cache, value_cache, out_weight)


def solution(mesh):
    in_specs = (
        P("rep", "head"),
        P(("rep", "seq", "sub"), None, "head"),
        P(("rep", "seq", "sub"), None, "head"),
        P("rep"),
        P(("rep", "seq", "sub")),
        P(("rep", "seq", "sub")),
        P("head", ("seq", "sub")),
    )
    return jax.shard_map(
        functools.partial(on_device, dict(mesh.shape)),
        mesh=mesh, in_specs=in_specs, out_specs=P("rep", ("seq", "sub")), check_vma=False,
    )
```

time: 79.1 us -> 24.7 us (0.31)
  blocking collectives: 50.9 us -> 0 us
  Pallas kernels: 0 us -> 23.2 us
  matrix products: 17.5 us -> 0 us
  other arithmetic: 6.07 us -> 0 us
  local copies, waits for them, and re-layouts: 4.05 us -> 1.3 us
    all_gather x3 -> x0, blocking collectives: 42.2 us -> none  [merged(): gathered = jax.tree.map(lambda a: lax.all_gather(a, axis), part)]
    pallas_call x0 -> x1, Pallas kernels: none -> 23.2 us  [on_device(): pl.pallas_call(functools.partial(kernel, pn), out_shape=jax.ShapeDtypeStr...]
    dot_general x5 -> x0, matrix products: 17.5 us -> none  [the longest x1 7.04 us: on_device(): jnp.einsum('sgjd,stgd->sgjt', picked, key_tiles, preferred_element_type=j...]
    psum x1 -> x0, blocking collectives: 8.73 us -> none  [on_device(): return lax.psum(partial_out, 'head').astype(jnp.bfloat16)]
    min x1 -> x0, other arithmetic: 3.19 us -> none  [on_device(): jnp.clip(jnp.take(seq_lengths, slot_owner, axis=0) - slot_page * PAGE, 0,...]
    gather x4 -> x0, local copies, waits for them, and re-layouts: 3.02 us -> none  [the longest x1 1.45 us: on_device(): jnp.take(seq_lengths, slot_owner, axis=0) - slot_page * PAGE]
    unnamed x6 -> x1, local copies, waits for them, and re-layouts: 0.17 us -> 1.3 us
    add x14 -> x0, other arithmetic: 1.09 us -> none  [the longest x7 0.92 us: merge_states(): spread(out_first, scale_first) + spread(out_second, scale_second)]
where the time goes in v1:
time: 24.7 us; the launch traced here: 24.5 us
  Pallas kernels  23.2 us (94%)
  local copies, waits for them, and re-layouts  1.3 us (5%)
    pallas_call x1, Pallas kernels, on_device(): pl.pallas_call(functools.partial(kernel, pn), out_shape=jax.ShapeDtypeStr...  23.2 us
    unnamed x1, local copies, waits for them, and re-layouts  1.3 us

profile of v1, /device:TPU:0, one launch (start us, length us, event | category | flops | bytes accessed | tf_op | source)
XLA Modules:
  0.0 24.5 jit_solution(3367842029831014397)
XLA Ops:
  0.0 23.2 %shard_map.73 = bf16[4,1024]{1,0:T(4,128)(2,1)} custom-call(s32[4]{0:T(128)} %lengths.1, s32[64]{0:T(128)} %owners.1, s32[64]{0:T(128)} %numbers.1, bf16[4,4096]{1,0:T(4,128)(2,1)} %q_ref.1, bf16[64,128,512]{2,1,0:T(8,128)(2,1)} %k_hbm.1, bf16[64,128,512]{2,1,0:T(8,128)(2,1)} %v_hbm.1, bf16[4096,1024]{1,0:T(8,128)(2,1)} %w_hbm.1), custom_call_target="tpu_custom_call" | custom-call | tf_op jit(solution)/shard_map/pallas_call | solution.py:239
  23.2 1.3 %copy.9 = bf16[4,1024]{1,0:T(4,128)(2,1)} copy(bf16[4,1024]{1,0:T(4,128)(2,1)} %shard_map.73) | data formatting | bytes 16384

commit v2 on v1

v2 whole, which is shorter than its diff:
```python
import functools

import jax
import jax.numpy as jnp
from jax import lax
from jax.experimental import pallas as pl
from jax.experimental.pallas import tpu as pltpu
from jax.sharding import PartitionSpec as P

DH = 128
NEG = -1e30
MESH = pl.DeviceIdType.MESH


class Plan:
    def __init__(self, mesh_shape, q_shape, k_shape, w_shape):
        self.seq, self.sub, self.head = (mesh_shape[a] for a in ("seq", "sub", "head"))
        self.peers = self.seq * self.sub
        self.batch = q_shape[0]
        self.pages, self.page, self.width = k_shape
        self.groups = self.width // DH
        self.per_group = q_shape[1] // self.width
        self.unit_groups = 2 if self.groups % 2 == 0 else 1
        self.units = self.groups // self.unit_groups
        self.unit_heads = self.unit_groups * self.per_group
        self.unit_width = self.unit_groups * DH
        self.rows = self.batch * self.unit_heads
        self.lanes = max(128, self.rows)
        self.window = 5
        self.chunk = min(16, self.pages)
        self.chunks = self.pages // self.chunk
        self.span = self.chunk * self.page
        self.columns = w_shape[1]
        self.depth = self.unit_heads * DH


def kernel(
    pn,
    lengths, owners, numbers,
    q_ref, k_hbm, v_hbm, w_hbm,
    out_ref,
    kbuf, vbuf, wbuf, scores, qf, qb, att,
    probs, orecv, srecv, parts,
    ksem, vsem, wsem, osem_s, osem_r, ssem_s, ssem_r, psem_s, psem_r,
):
    i_seq, i_sub, i_head = (lax.axis_index(a) for a in ("seq", "sub", "head"))
    me = i_seq * pn.sub + i_sub
    n = pn.peers

    def k_copy(u, c):
        at = (pl.ds(c * pn.chunk, pn.chunk), slice(None), pl.ds(u * pn.unit_width, pn.unit_width))
        return pltpu.make_async_copy(k_hbm.at[at], kbuf.at[at], ksem.at[u, c])

    def v_copy(u, c):
        at = (pl.ds(c * pn.chunk, pn.chunk), slice(None), pl.ds(u * pn.unit_width, pn.unit_width))
        return pltpu.make_async_copy(v_hbm.at[at], vbuf.at[at], vsem.at[u, c])

    def w_copy(u):
        at = pl.ds(u * pn.depth, pn.depth)
        return pltpu.make_async_copy(w_hbm.at[at], wbuf.at[at], wsem.at[u])

    order = []
    for u in range(pn.units):
        order += [k_copy(u, c) for c in range(pn.chunks)]
    for u in range(pn.units):
        order += [v_copy(u, c) for c in range(pn.chunks)]
    order += [w_copy(u) for u in range(pn.units)]
    reads = pn.units * pn.chunks * 2

    for copy in order[:pn.window]:
        copy.start()

    def arrive(at):
        order[at].wait()
        if at + pn.window < reads:
            order[at + pn.window].start()
        elif at + pn.window == reads:
            for copy in order[reads:]:
                copy.start()

    barrier = pltpu.get_barrier_semaphore()
    for axis, size, index in (("seq", pn.seq, i_seq), ("sub", pn.sub, i_sub), ("head", pn.head, i_head)):
        for k in range(1, size):
            pl.semaphore_signal(
                barrier, inc=1, device_id={axis: lax.rem(index + k, size)}, device_id_type=MESH
            )

    qf[...] = jnp.zeros_like(qf)
    for u in range(pn.units):
        for h in range(pn.unit_heads):
            g = h // pn.per_group
            col = (u * pn.unit_heads + h) * DH
            qf[u, g, pl.ds(h, pn.batch, stride=pn.unit_heads), :] = q_ref[
                :, pl.ds(col, DH)
            ].astype(jnp.float32)
    for u in range(pn.units):
        for g in range(pn.unit_groups):
            qb[u, :, pl.ds(g * DH, DH)] = qf[u, g].astype(jnp.bfloat16)
    scale = 1.0 / (DH**0.5)

    def place(k_seq, k_sub):
        return lax.rem(i_seq + k_seq, pn.seq), lax.rem(i_sub + k_sub, pn.sub)

    def spot_of(k_seq, k_sub):
        a, b = place(k_seq, k_sub)
        return a * pn.sub + b

    def o_copy(u, k_seq, k_sub):
        target = place(k_seq if k_sub == 0 else 0, k_sub)
        slot = me if k_sub == 0 else spot_of(-k_seq + pn.seq, 0)
        return pltpu.make_async_remote_copy(
            src_ref=orecv.at[u, slot], dst_ref=orecv.at[u, slot],
            send_sem=osem_s.at[u, k_seq * pn.sub + k_sub],
            recv_sem=osem_r.at[u, k_seq * pn.sub + k_sub],
            device_id={"seq": target[0], "sub": target[1]}, device_id_type=MESH,
        )

    def s_copy(u, k_seq, k_sub):
        target = place(k_seq if k_sub == 0 else 0, k_sub)
        slot = me if k_sub == 0 else spot_of(-k_seq + pn.seq, 0)
        return pltpu.make_async_remote_copy(
            src_ref=srecv.at[u, slot], dst_ref=srecv.at[u, slot],
            send_sem=ssem_s.at[u, k_seq * pn.sub + k_sub],
            recv_sem=ssem_r.at[u, k_seq * pn.sub + k_sub],
            device_id={"seq": target[0], "sub": target[1]}, device_id_type=MESH,
        )

    page_spot = lax.broadcasted_iota(jnp.int32, (pn.unit_heads, pn.page), 1)
    limits = []
    for p in range(pn.pages):
        owner = owners[p]
        valid = jnp.clip(lengths[owner] - numbers[p] * pn.page, 0, pn.page)
        limits.append((owner, valid))
    tops = [jnp.full((pn.rows, pn.page), NEG, jnp.float32) for _ in range(pn.units)]
    peaks = [None] * pn.units
    masses = [jnp.zeros((pn.rows, pn.page), jnp.float32) for _ in range(pn.units)]
    totals = [jnp.zeros((pn.rows, pn.unit_width), jnp.float32) for _ in range(pn.units)]

    def tile(buffer, u, c):
        cols = pl.ds(u * pn.unit_width, pn.unit_width)
        return buffer[pl.ds(c * pn.chunk, pn.chunk), :, cols].reshape(pn.span, pn.unit_width)

    def score_dot(u, c):
        scores[u, c] = lax.dot_general(
            qb[u], tile(kbuf, u, c), (((1,), (1,)), ((), ())), preferred_element_type=jnp.float32
        )

    def post(u, c):
        for p in range(pn.chunk):
            owner, valid = limits[c * pn.chunk + p]
            at = pl.ds(p * pn.page, pn.page)
            blocks = []
            for b in range(pn.batch):
                limit = jnp.where(owner == b, valid, 0)
                rows = pl.ds(b * pn.unit_heads, pn.unit_heads)
                blocks.append(jnp.where(page_spot < limit, scores[u, c, rows, at] * scale, NEG))
            piece = jnp.concatenate(blocks, axis=0)
            tops[u] = jnp.maximum(tops[u], piece)
            scores[u, c, :, at] = piece
        if c == pn.chunks - 1:
            peaks[u] = jnp.max(tops[u], axis=1, keepdims=True)

    def soften(u, c):
        for p in range(pn.chunk):
            at = pl.ds(p * pn.page, pn.page)
            block = jnp.exp(scores[u, c, :, at] - peaks[u]).astype(jnp.bfloat16)
            probs[u, c, :, at] = block
            masses[u] = masses[u] + block.astype(jnp.float32)

    def value_dot(u, c):
        totals[u] = totals[u] + jnp.dot(
            probs[u, c], tile(vbuf, u, c), preferred_element_type=jnp.float32
        )

    def finish(u):
        mass = jnp.sum(masses[u], axis=1, keepdims=True)
        level = peaks[u] + jnp.log(mass)
        blocks = []
        for b in range(pn.batch):
            for g in range(pn.unit_groups):
                r = b * pn.unit_heads + g * pn.per_group
                blocks.append(totals[u][r:r + pn.per_group, g * DH:(g + 1) * DH])
        mine = (jnp.concatenate(blocks, axis=0) / mass).astype(jnp.bfloat16)
        line = jnp.transpose(jnp.broadcast_to(level, (pn.rows, 128)))[0:1, :]
        if pn.rows < pn.lanes:
            line = jnp.concatenate([line, jnp.zeros((1, pn.lanes - pn.rows), jnp.float32)], axis=1)
        srecv[u, me] = line
        orecv[u, me] = mine

    def send(u):
        if u == 0:
            pl.semaphore_wait(barrier, pn.seq + pn.sub + pn.head - 3)
        for k in range(1, pn.seq):
            s_copy(u, k, 0).start()
            o_copy(u, k, 0).start()
        for k in range(1, pn.sub):
            s_copy(u, 0, k).start()
            o_copy(u, 0, k).start()

    def relay(u):
        for k in range(1, pn.seq):
            s_copy(u, k, 0).wait_recv()
            for j in range(1, pn.sub):
                s_copy(u, k, j).start()
            o_copy(u, k, 0).wait_recv()
            for j in range(1, pn.sub):
                o_copy(u, k, j).start()

    def merge(u):
        for k in range(pn.seq):
            for j in range(1, pn.sub):
                s_copy(u, k, j).wait_recv()
                o_copy(u, k, j).wait_recv()
        level = srecv[u].reshape(n, pn.lanes)
        weight = jnp.exp(level - jnp.max(level, axis=0, keepdims=True))
        weight = weight / jnp.sum(weight, axis=0, keepdims=True)
        turned = jnp.transpose(weight)
        total = None
        for s in range(n):
            term = orecv[u, s].astype(jnp.float32) * turned[0:pn.rows, s:s + 1]
            total = term if total is None else total + term
        att[u] = total
        heads = [att[u, pl.ds(h, pn.batch, stride=pn.unit_heads), :] for h in range(pn.unit_heads)]
        return jnp.concatenate(heads, axis=1).astype(jnp.bfloat16)

    soften_at = {}
    for u in range(pn.units):
        for c in range(pn.chunks):
            step = min((u + 1) * pn.chunks + 1 + c, (pn.units + u) * pn.chunks + c)
            soften_at.setdefault(step, []).append((u, c))
    for step in range(2 * pn.units * pn.chunks):
        arrive(step)
        u, c = divmod(step, pn.chunks)
        if 1 <= step <= pn.units * pn.chunks:
            post(*divmod(step - 1, pn.chunks))
        if u < pn.units:
            score_dot(u, c)
        for item in soften_at.get(step, ()):
            soften(*item)
        if u >= pn.units:
            if c == 0 and u > pn.units:
                finish(u - pn.units - 1)
            value_dot(u - pn.units, c)
            if c == 0 and u > pn.units:
                send(u - pn.units - 1)
    finish(pn.units - 1)
    send(pn.units - 1)

    total = jnp.zeros((pn.batch, pn.columns), jnp.float32)
    relay(0)
    for u in range(pn.units):
        order[reads + u].wait()
        if u > 0:
            relay(u)
        rows = merge(u)
        total = total + jnp.dot(
            rows, wbuf[pl.ds(u * pn.depth, pn.depth), :], preferred_element_type=jnp.float32
        )
    parts[i_head] = total

    def p_copy(k):
        return pltpu.make_async_remote_copy(
            src_ref=parts.at[i_head], dst_ref=parts.at[i_head],
            send_sem=psem_s.at[k], recv_sem=psem_r.at[k],
            device_id={"head": lax.rem(i_head + k, pn.head)}, device_id_type=MESH,
        )

    for k in range(1, pn.head):
        p_copy(k).start()
    for u in range(pn.units):
        for k in range(1, n):
            s_copy(u, *divmod(k, pn.sub)).wait_send()
            o_copy(u, *divmod(k, pn.sub)).wait_send()
    for k in range(1, pn.head):
        p_copy(k).wait()
    result = parts[0]
    for s in range(1, pn.head):
        result = result + parts[s]
    out_ref[...] = result.astype(out_ref.dtype)


def on_device(mesh_shape, queries, key_cache, value_cache, seq_lengths, slot_owner, slot_page, out_weight):
    pn = Plan(mesh_shape, queries.shape, key_cache.shape, out_weight.shape)
    smem = pl.BlockSpec(memory_space=pltpu.SMEM)
    vmem = pl.BlockSpec(memory_space=pltpu.VMEM)
    anywhere = pl.BlockSpec(memory_space=pl.ANY)
    n, u = pn.peers, pn.units
    dma = pltpu.SemaphoreType.DMA
    return pl.pallas_call(
        functools.partial(kernel, pn),
        out_shape=jax.ShapeDtypeStruct((pn.batch, pn.columns), queries.dtype),
        in_specs=[smem, smem, smem, vmem, anywhere, anywhere, anywhere],
        out_specs=vmem,
        scratch_shapes=[
            pltpu.VMEM(key_cache.shape, key_cache.dtype),
            pltpu.VMEM(value_cache.shape, value_cache.dtype),
            pltpu.VMEM(out_weight.shape, out_weight.dtype),
            pltpu.VMEM((u, pn.chunks, pn.rows, pn.span), jnp.float32),
            pltpu.VMEM((u, pn.unit_groups, pn.rows, DH), jnp.float32),
            pltpu.VMEM((u, pn.rows, pn.unit_width), jnp.bfloat16),
            pltpu.VMEM((u, pn.rows, DH), jnp.float32),
            pltpu.VMEM((u, pn.chunks, pn.rows, pn.span), jnp.bfloat16),
            pltpu.VMEM((u, n, pn.rows, DH), jnp.bfloat16),
            pltpu.VMEM((u, n, 1, pn.lanes), jnp.float32),
            pltpu.VMEM((pn.head, pn.batch, pn.columns), jnp.float32),
            dma((u, pn.chunks)), dma((u, pn.chunks)), dma((u,)),
            dma((u, n)), dma((u, n)), dma((u, n)), dma((u, n)),
            dma((pn.head,)), dma((pn.head,)),
        ],
        compiler_params=pltpu.CompilerParams(
            collective_id=0, has_side_effects=True, vmem_limit_bytes=60 * 1024 * 1024
        ),
    )(seq_lengths, slot_owner, slot_page, queries, key_cache, value_cache, out_weight)


def solution(mesh):
    in_specs = (
        P("rep", "head"),
        P(("rep", "seq", "sub"), None, "head"),
        P(("rep", "seq", "sub"), None, "head"),
        P("rep"),
        P(("rep", "seq", "sub")),
        P(("rep", "seq", "sub")),
        P("head", ("seq", "sub")),
    )
    return jax.shard_map(
        functools.partial(on_device, dict(mesh.shape)),
        mesh=mesh, in_specs=in_specs, out_specs=P("rep", ("seq", "sub")), check_vma=False,
    )
```

time: 24.7 us -> 24.7 us (level)
  no operation moved by 1% of the time
where the time goes in v2:
time: 24.7 us; the launch traced here: 24.5 us
  Pallas kernels  23.2 us (94%)
  local copies, waits for them, and re-layouts  1.3 us (5%)
    pallas_call x1, Pallas kernels, on_device(): pl.pallas_call(functools.partial(kernel, pn), out_shape=jax.ShapeDtypeStr...  23.2 us
    unnamed x1, local copies, waits for them, and re-layouts  1.3 us

profile of v2, /device:TPU:0, one launch (start us, length us, event | category | flops | bytes accessed | tf_op | source)
XLA Modules:
  0.0 24.5 jit_solution(384314733027986640)
XLA Ops:
  0.0 23.2 %shard_map.73 = bf16[4,1024]{1,0:T(4,128)(2,1)} custom-call(s32[4]{0:T(128)} %lengths.1, s32[64]{0:T(128)} %owners.1, s32[64]{0:T(128)} %numbers.1, bf16[4,4096]{1,0:T(4,128)(2,1)} %q_ref.1, bf16[64,128,512]{2,1,0:T(8,128)(2,1)} %k_hbm.1, bf16[64,128,512]{2,1,0:T(8,128)(2,1)} %v_hbm.1, bf16[4096,1024]{1,0:T(8,128)(2,1)} %w_hbm.1), custom_call_target="tpu_custom_call" | custom-call | tf_op jit(solution)/shard_map/pallas_call | solution.py:289
  23.2 1.3 %copy.9 = bf16[4,1024]{1,0:T(4,128)(2,1)} copy(bf16[4,1024]{1,0:T(4,128)(2,1)} %shard_map.73) | data formatting | bytes 16384

commit v3 on v2

v3 whole, which is shorter than its diff:
```python
import functools

import jax
import jax.numpy as jnp
from jax import lax
from jax.experimental import pallas as pl
from jax.experimental.pallas import tpu as pltpu
from jax.sharding import PartitionSpec as P

DH = 128
NEG = -1e30
MESH = pl.DeviceIdType.MESH


class Plan:
    def __init__(self, mesh_shape, q_shape, k_shape, w_shape):
        self.seq, self.sub, self.head = (mesh_shape[a] for a in ("seq", "sub", "head"))
        self.peers = self.seq * self.sub
        self.batch = q_shape[0]
        self.pages, self.page, self.width = k_shape
        self.groups = self.width // DH
        self.per_group = q_shape[1] // self.width
        self.unit_groups = 2 if self.groups % 2 == 0 else 1
        self.units = self.groups // self.unit_groups
        self.unit_heads = self.unit_groups * self.per_group
        self.unit_width = self.unit_groups * DH
        self.rows = self.batch * self.unit_heads
        self.group_rows = self.batch * self.per_group
        self.lanes = max(128, self.group_rows)
        self.window = 5
        self.chunk = min(16, self.pages)
        self.chunks = self.pages // self.chunk
        self.span = self.chunk * self.page
        self.columns = w_shape[1]
        self.depth = self.per_group * DH
        self.relayed = self.groups // 2
        self.value_chunk = min(32, self.pages)
        self.value_chunks = self.pages // self.value_chunk
        self.value_span = self.value_chunk * self.page


def kernel(
    pn,
    lengths, owners, numbers,
    q_ref, k_hbm, v_hbm, w_hbm,
    out_ref,
    kbuf, vbuf, wbuf, scores, qf, qb, att,
    probs, orecv, srecv, parts,
    ksem, vsem, wsem, osem_s, osem_r, ssem_s, ssem_r, psem_s, psem_r,
):
    i_seq, i_sub, i_head = (lax.axis_index(a) for a in ("seq", "sub", "head"))
    me = i_seq * pn.sub + i_sub
    n = pn.peers

    def k_copy(u, c):
        at = (pl.ds(c * pn.chunk, pn.chunk), slice(None), pl.ds(u * pn.unit_width, pn.unit_width))
        return pltpu.make_async_copy(k_hbm.at[at], kbuf.at[at], ksem.at[u, c])

    def v_copy(u, c):
        at = (pl.ds(c * pn.value_chunk, pn.value_chunk), slice(None), pl.ds(u * DH, DH))
        return pltpu.make_async_copy(v_hbm.at[at], vbuf.at[at], vsem.at[u, c])

    def w_copy(u):
        at = pl.ds(u * pn.depth, pn.depth)
        return pltpu.make_async_copy(w_hbm.at[at], wbuf.at[at], wsem.at[u])

    order = []
    for u in range(pn.units):
        order += [k_copy(u, c) for c in range(pn.chunks)]
    for g in range(pn.groups):
        order += [v_copy(g, c) for c in range(pn.value_chunks)]
    order += [w_copy(g) for g in range(pn.groups)]
    score_steps = pn.units * pn.chunks
    reads = score_steps + pn.groups * pn.value_chunks

    for copy in order[:pn.window]:
        copy.start()

    def arrive(at):
        order[at].wait()
        if at + pn.window < reads:
            order[at + pn.window].start()
        elif at + pn.window == reads:
            for copy in order[reads:]:
                copy.start()

    barrier = pltpu.get_barrier_semaphore()
    for k in range(1, n):
        k_seq, k_sub = divmod(k, pn.sub)
        who = {"seq": lax.rem(i_seq + k_seq, pn.seq), "sub": lax.rem(i_sub + k_sub, pn.sub)}
        pl.semaphore_signal(barrier, inc=1, device_id=who, device_id_type=MESH)
    for k in range(1, pn.head):
        who = {"head": lax.rem(i_head + k, pn.head)}
        pl.semaphore_signal(barrier, inc=1, device_id=who, device_id_type=MESH)

    qf[...] = jnp.zeros_like(qf)
    for u in range(pn.units):
        for h in range(pn.unit_heads):
            g = h // pn.per_group
            col = (u * pn.unit_heads + h) * DH
            qf[u, g, pl.ds(g * pn.group_rows + h % pn.per_group, pn.batch, stride=pn.per_group), :] = q_ref[
                :, pl.ds(col, DH)
            ].astype(jnp.float32)
    for u in range(pn.units):
        for g in range(pn.unit_groups):
            qb[u, :, pl.ds(g * DH, DH)] = qf[u, g].astype(jnp.bfloat16)
    scale = 1.0 / (DH**0.5)

    def remote(ref, g, k, send_sem, recv_sem):
        k_seq, k_sub = divmod(k, pn.sub)
        hop, slot = k_seq, me
        if g < pn.relayed and k_sub > 0:
            hop = 0
            if k_seq > 0:
                slot = lax.rem(i_seq + pn.seq - k_seq, pn.seq) * pn.sub + i_sub
        return pltpu.make_async_remote_copy(
            src_ref=ref.at[g, slot], dst_ref=ref.at[g, slot],
            send_sem=send_sem.at[g, k], recv_sem=recv_sem.at[g, k],
            device_id={
                "seq": lax.rem(i_seq + hop, pn.seq),
                "sub": lax.rem(i_sub + k_sub, pn.sub),
            },
            device_id_type=MESH,
        )

    def o_copy(g, k):
        return remote(orecv, g, k, osem_s, osem_r)

    def s_copy(g, k):
        return remote(srecv, g, k, ssem_s, ssem_r)

    page_spot = lax.broadcasted_iota(jnp.int32, (pn.per_group, pn.page), 1)
    limits = []
    for p in range(pn.pages):
        owner = owners[p]
        valid = jnp.clip(lengths[owner] - numbers[p] * pn.page, 0, pn.page)
        limits.append((owner, valid))
    tops = [jnp.full((pn.rows, pn.page), NEG, jnp.float32) for _ in range(pn.units)]
    peaks = [None] * pn.units
    masses = [jnp.zeros((pn.group_rows, pn.page), jnp.float32) for _ in range(pn.groups)]
    totals = [jnp.zeros((pn.group_rows, DH), jnp.float32) for _ in range(pn.groups)]

    def score_dot(u, c):
        cols = pl.ds(u * pn.unit_width, pn.unit_width)
        keys = kbuf[pl.ds(c * pn.chunk, pn.chunk), :, cols].reshape(pn.span, pn.unit_width)
        scores[u, c] = lax.dot_general(
            qb[u], keys, (((1,), (1,)), ((), ())), preferred_element_type=jnp.float32
        )

    def post(u, c):
        for p in range(pn.chunk):
            owner, valid = limits[c * pn.chunk + p]
            at = pl.ds(p * pn.page, pn.page)
            blocks = []
            live = [page_spot < jnp.where(owner == b, valid, 0) for b in range(pn.batch)]
            for r in range(pn.unit_groups * pn.batch):
                rows = pl.ds(r * pn.per_group, pn.per_group)
                blocks.append(jnp.where(live[r % pn.batch], scores[u, c, rows, at] * scale, NEG))
            piece = jnp.concatenate(blocks, axis=0)
            tops[u] = jnp.maximum(tops[u], piece)
            scores[u, c, :, at] = piece
        if c == pn.chunks - 1:
            peaks[u] = jnp.max(tops[u], axis=1, keepdims=True)

    def soften(g, c):
        u, part = divmod(g, pn.unit_groups)
        rows = slice(part * pn.group_rows, (part + 1) * pn.group_rows)
        peak = peaks[u][rows]
        for p in range(pn.value_chunk):
            from_chunk, spot = divmod(c * pn.value_chunk + p, pn.chunk)
            block = jnp.exp(scores[u, from_chunk, rows, pl.ds(spot * pn.page, pn.page)] - peak)
            block = block.astype(jnp.bfloat16)
            probs[g, c, :, pl.ds(p * pn.page, pn.page)] = block
            masses[g] = masses[g] + block.astype(jnp.float32)

    def value_dot(g, c):
        values = vbuf[pl.ds(c * pn.value_chunk, pn.value_chunk), :, pl.ds(g * DH, DH)]
        totals[g] = totals[g] + jnp.dot(
            probs[g, c], values.reshape(pn.value_span, DH), preferred_element_type=jnp.float32
        )

    def finish(g):
        u, part = divmod(g, pn.unit_groups)
        mass = jnp.sum(masses[g], axis=1, keepdims=True)
        level = peaks[u][part * pn.group_rows:(part + 1) * pn.group_rows] + jnp.log(mass)
        line = jnp.transpose(jnp.broadcast_to(level, (pn.group_rows, 128)))[0:1, :]
        if pn.group_rows < pn.lanes:
            pad = jnp.zeros((1, pn.lanes - pn.group_rows), jnp.float32)
            line = jnp.concatenate([line, pad], axis=1)
        srecv[g, me] = line
        orecv[g, me] = (totals[g] / mass).astype(jnp.bfloat16)

    def send(u):
        if u == 0:
            pl.semaphore_wait(barrier, n - 1 + pn.head - 1)
        for k in [*range(pn.sub, n), *range(1, pn.sub)]:
            if k < pn.sub or u >= pn.relayed or k % pn.sub == 0:
                s_copy(u, k).start()
                o_copy(u, k).start()

    def relay(u):
        for k in range(pn.sub, n, pn.sub):
            s_copy(u, k).wait_recv()
            o_copy(u, k).wait_recv()
            for j in range(1, pn.sub):
                s_copy(u, k + j).start()
                o_copy(u, k + j).start()

    def merge(u):
        for k in range(1, n):
            if u >= pn.relayed or k % pn.sub > 0:
                s_copy(u, k).wait_recv()
                o_copy(u, k).wait_recv()
        level = srecv[u].reshape(n, pn.lanes)
        weight = jnp.exp(level - jnp.max(level, axis=0, keepdims=True))
        weight = weight / jnp.sum(weight, axis=0, keepdims=True)
        turned = jnp.transpose(weight)
        total = None
        for s in range(n):
            term = orecv[u, s].astype(jnp.float32) * turned[0:pn.group_rows, s:s + 1]
            total = term if total is None else total + term
        att[u] = total
        heads = [att[u, pl.ds(h, pn.batch, stride=pn.per_group), :] for h in range(pn.per_group)]
        return jnp.concatenate(heads, axis=1).astype(jnp.bfloat16)

    soften_at = {}
    for g in range(pn.groups):
        for c in range(pn.value_chunks):
            needed = score_steps + g * pn.value_chunks + c
            ready = (g // pn.unit_groups + 1) * pn.chunks + 1
            soften_at.setdefault(max(ready, needed - 1) if ready <= needed else needed, []).append((g, c))
    for step in range(reads):
        arrive(step)
        if 1 <= step <= score_steps:
            post(*divmod(step - 1, pn.chunks))
        if step < score_steps:
            score_dot(*divmod(step, pn.chunks))
        for item in soften_at.get(step, ()):
            soften(*item)
        if step >= score_steps:
            g, c = divmod(step - score_steps, pn.value_chunks)
            if c == 0 and g > 0:
                finish(g - 1)
            value_dot(g, c)
            if c == 0 and g > 0:
                send(g - 1)
    finish(pn.groups - 1)
    send(pn.groups - 1)

    for g in range(pn.relayed):
        relay(g)
    total = jnp.zeros((pn.batch, pn.columns), jnp.float32)
    for g in range(pn.groups):
        order[reads + g].wait()
        rows = merge(g)
        total = total + jnp.dot(
            rows, wbuf[pl.ds(g * pn.depth, pn.depth), :], preferred_element_type=jnp.float32
        )
    parts[i_head] = total

    def p_copy(k):
        return pltpu.make_async_remote_copy(
            src_ref=parts.at[i_head], dst_ref=parts.at[i_head],
            send_sem=psem_s.at[k], recv_sem=psem_r.at[k],
            device_id={"head": lax.rem(i_head + k, pn.head)}, device_id_type=MESH,
        )

    for k in range(1, pn.head):
        p_copy(k).start()
    for u in range(pn.groups):
        for k in range(1, n):
            s_copy(u, k).wait_send()
            o_copy(u, k).wait_send()
    for k in range(1, pn.head):
        p_copy(k).wait()
    result = parts[0]
    for s in range(1, pn.head):
        result = result + parts[s]
    out_ref[...] = result.astype(out_ref.dtype)


def on_device(mesh_shape, queries, key_cache, value_cache, seq_lengths, slot_owner, slot_page, out_weight):
    pn = Plan(mesh_shape, queries.shape, key_cache.shape, out_weight.shape)
    smem = pl.BlockSpec(memory_space=pltpu.SMEM)
    vmem = pl.BlockSpec(memory_space=pltpu.VMEM)
    anywhere = pl.BlockSpec(memory_space=pl.ANY)
    n, u, g = pn.peers, pn.units, pn.groups
    dma = pltpu.SemaphoreType.DMA
    return pl.pallas_call(
        functools.partial(kernel, pn),
        out_shape=pltpu.VMEM((pn.batch, pn.columns), queries.dtype),
        in_specs=[smem, smem, smem, vmem, anywhere, anywhere, anywhere],
        out_specs=vmem,
        scratch_shapes=[
            pltpu.VMEM(key_cache.shape, key_cache.dtype),
            pltpu.VMEM(value_cache.shape, value_cache.dtype),
            pltpu.VMEM(out_weight.shape, out_weight.dtype),
            pltpu.VMEM((u, pn.chunks, pn.rows, pn.span), jnp.float32),
            pltpu.VMEM((u, pn.unit_groups, pn.rows, DH), jnp.float32),
            pltpu.VMEM((u, pn.rows, pn.unit_width), jnp.bfloat16),
            pltpu.VMEM((g, pn.group_rows, DH), jnp.float32),
            pltpu.VMEM((g, pn.value_chunks, pn.group_rows, pn.value_span), jnp.bfloat16),
            pltpu.VMEM((g, n, pn.group_rows, DH), jnp.bfloat16),
            pltpu.VMEM((g, n, 1, pn.lanes), jnp.float32),
            pltpu.VMEM((pn.head, pn.batch, pn.columns), jnp.float32),
            dma((u, pn.chunks)), dma((g, pn.value_chunks)), dma((g,)),
            dma((g, n)), dma((g, n)), dma((g, n)), dma((g, n)),
            dma((pn.head,)), dma((pn.head,)),
        ],
        compiler_params=pltpu.CompilerParams(
            collective_id=0, has_side_effects=True, vmem_limit_bytes=60 * 1024 * 1024
        ),
    )(seq_lengths, slot_owner, slot_page, queries, key_cache, value_cache, out_weight)


def solution(mesh):
    in_specs = (
        P("rep", "head"),
        P(("rep", "seq", "sub"), None, "head"),
        P(("rep", "seq", "sub"), None, "head"),
        P("rep"),
        P(("rep", "seq", "sub")),
        P(("rep", "seq", "sub")),
        P("head", ("seq", "sub")),
    )
    return jax.shard_map(
        functools.partial(on_device, dict(mesh.shape)),
        mesh=mesh, in_specs=in_specs, out_specs=P("rep", ("seq", "sub")), check_vma=False,
    )
```

time: 24.7 us -> 22.9 us (0.927)
  Pallas kernels: 23.2 us -> 22.1 us
  local copies, waits for them, and re-layouts: 1.3 us -> 0.6 us
    pallas_call x1, Pallas kernels: 23.2 us -> 22.1 us  [on_device(): pl.pallas_call(functools.partial(kernel, pn), out_shape=pltpu.VMEM((pn.ba...]
    unnamed x1, local copies, waits for them, and re-layouts: 1.3 us -> 0.6 us
where the time goes in v3:
time: 22.9 us; the launch traced here: 22.7 us
  Pallas kernels  22.1 us (97%)
  local copies, waits for them, and re-layouts  0.6 us (3%)
    pallas_call x1, Pallas kernels, on_device(): pl.pallas_call(functools.partial(kernel, pn), out_shape=pltpu.VMEM((pn.ba...  22.1 us
    unnamed x1, local copies, waits for them, and re-layouts  0.6 us

profile of v3, /device:TPU:0, one launch (start us, length us, event | category | flops | bytes accessed | tf_op | source)
XLA Modules:
  0.0 22.7 jit_solution(1755805628989805642)
XLA Ops:
  0.0 22.1 %shard_map.73 = bf16[4,1024]{1,0:T(4,128)(2,1)S(1)} custom-call(s32[4]{0:T(128)} %lengths.1, s32[64]{0:T(128)} %owners.1, s32[64]{0:T(128)} %numbers.1, bf16[4,4096]{1,0:T(4,128)(2,1)} %q_ref.1, bf16[64,128,512]{2,1,0:T(8,128)(2,1)} %k_hbm.1, bf16[64,128,512]{2,1,0:T(8,128)(2,1)} %v_hbm.1, bf16[4096,1024]{1,0:T(8,128)(2,1)} %w_hbm.1), custom_call_target="tpu_custom_call" | custom-call | tf_op jit(solution)/shard_map/pallas_call | solution.py:289
  22.1 0.6 %copy.9 = bf16[4,1024]{1,0:T(4,128)(2,1)} copy(bf16[4,1024]{1,0:T(4,128)(2,1)S(1)} %shard_map.73) | data formatting | bytes 16384
